TPU v7x, 128 devices: a whole 4x4x4 slice. The times are simulated.
128 devices in a mesh: seq: 16 (over y, z_lo, core), tensor: 8 (over z_hi, x).
Axes of the slice: x: 4, y: 4, z: 4 (z_hi: 2, z_lo: 2; z = z_hi * 2 + z_lo), core: 2. Of those that a mesh axis runs over, the one named last changes fastest.
Arguments:
- tokens: bfloat16 [8192, 8192], P('seq', 'tensor'), may hold values from -6 to 6
- positions: int32 [8192], P('seq'), may hold values from 0 to 8191, each once
- norm_gain: float32 [8192], replicated, may hold values from 0.1 to 1.9
- w_query: bfloat16 [8192, 4096], P('seq', 'tensor'), may hold values from -0.0625 to 0.0625
- w_key: bfloat16 [8192, 1024], P('seq', 'tensor'), may hold values from -0.0625 to 0.0625
- w_value: bfloat16 [8192, 1024], P('seq', 'tensor'), may hold values from -0.0625 to 0.0625
- b_query: float32 [4096], P('tensor'), may hold values from -40 to 40
- b_key: float32 [1024], P('tensor'), may hold values from -40 to 40
- b_value: float32 [1024], P('tensor'), may hold values from -6 to 6
- w_out: bfloat16 [4096, 8192], P('tensor', 'seq'), may hold values from -0.09375 to 0.09375
Outputs:
- mixed: bfloat16 [8192, 8192], P('seq', 'tensor')
- context: bfloat16 [8192, 4096], P('seq', 'tensor')
Inputs may be any that keep to these rules, and one draw needn't show every extreme that they name: positions holds every position 0 to 8191 once.
All inputs are finite; a program needn't handle non-finite values.
Results may differ from a plain program's by a relative error of at most 0.025.
Values may be sent and summed in bfloat16 or wider, within the bound.
No kernel may reach another device: no remote copies, remote signals or barrier semaphores. Data moves between devices by JAX's collectives and lax.ppermute only.
A program may use at most 128 MiB of HBM per device.

v0:
```python
import math
import jax
import jax.numpy as jnp
from jax import lax
from jax.sharding import PartitionSpec as P

HD = 128
NORM_EPS = 1e-06
ROPE_BASE = 1000000.0
NEG_FILL = -1e30


def sent_together(arrays, axis, dim, along):
    ends, at = ([], 0)
    for a in arrays[:-1]:
        at += a.shape[along]
        ends.append(at)
    both = jnp.concatenate(arrays, axis=along)
    return tuple(jnp.split(lax.all_gather(both, axis, axis=dim, tiled=True), ends, axis=along))


def rotate(values_in, positions):
    half_dim = HD // 2
    inv_freq = ROPE_BASE ** (-jnp.arange(half_dim, dtype=jnp.float32) * 2.0 / HD)
    angles = positions.astype(jnp.float32)[:, None] * inv_freq[None, :]
    cosine = jnp.cos(angles)[:, None, :]
    sines = jnp.sin(angles)[:, None, :]
    lower_half = values_in[..., :half_dim]
    upper_half = values_in[..., half_dim:]
    return jnp.concatenate(
        [lower_half * cosine - upper_half * sines, upper_half * cosine + lower_half * sines], -1
    )


def shards(tokens, positions, norm_gain, w_query, w_key, w_value, b_query, b_key, b_value, w_out):
    tok_rows = tokens.shape[0]
    features = lax.all_gather(tokens, "tensor", axis=1, tiled=True)
    inputs = features.astype(jnp.float32)
    inverse_rms = lax.rsqrt(jnp.mean(inputs * inputs, -1, keepdims=True) + NORM_EPS)
    normed = (inputs * inverse_rms * norm_gain[None, :]).astype(jnp.bfloat16)
    w_cat = jnp.concatenate((w_query, w_key, w_value), 1)
    b_cat = jnp.concatenate((b_query, b_key, b_value))
    projected = jnp.dot(
        normed, lax.all_gather(w_cat, "seq", axis=0, tiled=True), preferred_element_type=jnp.float32
    )
    projected = projected + b_cat[None, :]
    query_cols = w_query.shape[1]
    key_cols = w_key.shape[1]
    heads_here = query_cols // HD
    kv_here = key_cols // HD
    group = heads_here // kv_here
    queries = rotate(projected[:, :query_cols].reshape(tok_rows, heads_here, HD), positions).astype(
        jnp.bfloat16
    )
    queries = queries.reshape(tok_rows, kv_here, group, HD)
    keys_rot = rotate(
        projected[:, query_cols : query_cols + key_cols].reshape(tok_rows, kv_here, HD), positions
    ).astype(jnp.bfloat16)
    values = (
        projected[:, query_cols + key_cols :].astype(jnp.bfloat16).reshape(tok_rows, kv_here, HD)
    )
    scale = HD ** (-0.5)

    def attend_block(running, key_block):
        running_max, denominator, numerator = running
        block_keys, block_values, key_pos = key_block
        scores = (
            jnp.einsum("tgcd,sgd->gcts", queries, block_keys, preferred_element_type=jnp.float32)
            * scale
        )
        allowed = (key_pos[None, :] <= positions[:, None])[None, None, :, :]
        scores = jnp.where(allowed, scores, NEG_FILL)
        new_max = jnp.maximum(running_max, jnp.max(scores, -1))
        weights = jnp.where(allowed, jnp.exp(scores - new_max[..., None]), 0.0)
        rescale = jnp.exp(running_max - new_max)
        denominator = denominator * rescale + jnp.sum(weights, -1)
        numerator = numerator * rescale[..., None] + jnp.einsum(
            "gcts,sgd->gctd",
            weights.astype(jnp.bfloat16),
            block_values,
            preferred_element_type=jnp.float32,
        )
        return (new_max, denominator, numerator)

    start_state = (
        jnp.full((kv_here, group, tok_rows), NEG_FILL, jnp.float32),
        jnp.zeros((kv_here, group, tok_rows), jnp.float32),
        jnp.zeros((kv_here, group, tok_rows, HD), jnp.float32),
    )
    all_keys_in, all_values_in, key_pos = (
        *sent_together((keys_rot, values), "seq", 0, 1),
        lax.all_gather(positions, "seq", axis=0, tiled=True),
    )
    count = all_keys_in.shape[0]
    width = math.gcd(count, 2048)
    stacked = (
        all_keys_in.reshape(count // width, width, kv_here, HD),
        all_values_in.reshape(count // width, width, kv_here, HD),
        key_pos.reshape(count // width, width),
    )

    def stepper(carried, key_block):
        return (attend_block(carried, key_block), None)

    result, unused = lax.scan(stepper, start_state, stacked)
    unused_max, denominator, numerator = result
    per_head = numerator / denominator[..., None]
    context = (
        jnp.transpose(per_head, (2, 0, 1, 3))
        .reshape(tok_rows, heads_here * HD)
        .astype(jnp.bfloat16)
    )
    out_terms = jnp.dot(
        context,
        lax.all_gather(w_out, "seq", axis=1, tiled=True),
        preferred_element_type=jnp.float32,
    )
    summed = lax.psum_scatter(
        out_terms.astype(jnp.bfloat16), "tensor", scatter_dimension=1, tiled=True
    ).astype(jnp.float32)
    mixed = (tokens.astype(jnp.float32) + summed).astype(jnp.bfloat16)
    return (mixed, context)


def solution(mesh):
    in_specs = (
        P("seq", "tensor"),
        P("seq"),
        P(),
        P("seq", "tensor"),
        P("seq", "tensor"),
        P("seq", "tensor"),
        P("tensor"),
        P("tensor"),
        P("tensor"),
        P("tensor", "seq"),
    )
    out_specs = (P("seq", "tensor"), P("seq", "tensor"))
    return jax.shard_map(shards, mesh=mesh, in_specs=in_specs, out_specs=out_specs, check_vma=False)
```

profile of v0, /device:TPU:0, one launch (start us, length us, event | category | flops | bytes accessed | tf_op | source)
XLA Modules:
  0.0 495.2 jit_solution(8700985036103313961)
XLA Ops:
  11.6 109.7 %all-gather.6.cloned.1.call-done = bf16[512,8192]{1,0:T(8,128)(2,1)} async-done(((bf16[512,1024]{1,0:T(8,128)(2,1)}), bf16[512,8192]{1,0:T(8,128)(2,1)}) %all-gather.6.cloned.1.call-update) | async-done | bytes 8388624 | tf_op jit(solution)/shard_map/all_gather | solution.py:37
  121.2 5.1 %fusion.25 = f32[512]{0:T(512)S(1)} fusion(bf16[512,8192]{1,0:T(8,128)(2,1)} %all-gather.6.cloned.1.call-done), kind=kLoop, calls=%fused_computation.31 | loop fusion | flops 12582400 | bytes 8390656 | tf_op jit(solution)/shard_map/reduce_sum | solution.py:39
  126.4 66.7 %all-gather.8.cloned.1.call-done = bf16[8192,768]{1,0:T(8,128)(2,1)} async-done(((bf16[512,768]{1,0:T(8,128)(2,1)}), bf16[8192,768]{1,0:T(8,128)(2,1)}) %all-gather.8.cloned.1.call-update) | async-done | bytes 12582928 | tf_op jit(solution)/shard_map/all_gather | solution.py:44
  193.1 12.5 %fusion.32 = f32[512,768]{0,1:T(8,128)S(1)} fusion(bf16[8192,768]{1,0:T(8,128)(2,1)} %all-gather.8.cloned.1.call-done, bf16[512,8192]{1,0:T(8,128)(2,1)} %all-gather.6.cloned.1.call-done, f32[8192]{0:T(1024)S(1)} %copy-done.5, f32[512]{0:T(512)S(1)} %add_rsqrt_fusion, f32[768]{0:T(1024)S(1)} %pad_maximum_fusion.3), kind=kOutput, calls=%fused_computation.39 | convolution fusion | flops 6459621376 | bytes 22582272 | tf_op jit(solution)/shard_map/dot_general | solution.py:43
  208.6 19.0 %all-gather = s32[16,1,512]{2,1,0:T(1,128)S(1)} all-gather(s32[1,1,512]{2,1,0:T(1,128)S(1)} %bitcast.114), channel_id=1, replica_groups=mesh['seq'=16,'tensor'=8] {'seq'}, dimensions={0}, use_global_device_ids=true | all-gather | bytes 34816 | tf_op jit(solution)/shard_map/all_gather | solution.py:92
  230.0 15.2 %all-gather.10.cloned.1.call-done = bf16[8192,2,128]{0,2,1:T(8,128)(2,1)} async-done(((bf16[512,2,128]{0,2,1:T(8,128)(2,1)}), bf16[8192,2,128]{0,2,1:T(8,128)(2,1)}) %all-gather.10.cloned.1.call-update) | async-done | bytes 4194320 | tf_op jit(solution)/shard_map/all_gather | solution.py:19
  245.2 3.9 fusion.47
  249.2 4.1 copy.33
  255.7 103.9 %while.15 = (s32[]{:T(128)}, f32[1,4,512]{2,1,0:T(4,128)S(1)}, f32[1,4,512]{2,1,0:T(4,128)S(1)}, f32[1,4,512,128]{3,2,1,0:T(8,128)S(1)}, s32[4,2048]{1,0:T(4,128...) while((s32[]{:T(128)}, f32[1,4,512]{2,1,0:T(4,128)S(1)}, ...), condition=%wide.region_4.5_spmd.clone, body=%wide.region_1.4_spmd.clone.sunk | while | flops 2203856896 | bytes 125463704 | solution.py:105
  256.5 10.1 %fusion.60 = (f32[4,512]{1,0:T(4,128)S(1)}, f32[2048,512,4]{1,0,2:T(8,128)}) fusion(pred[512,2048]{0,1:T(8,128)(4,1)S(1)} %broadcast_compare_fusion.2, bf16[512,1,4,128]{3,0,2,1:T(8,128)(2,1)} %get-tuple-element.233, bf16[4,2048,1,128]{3,1,2,0:T(8,128)(2,1)} %get-tuple-element.232, s32[]{:T(128)} %get-tuple-element.215), kind=kOutput, calls=%fused_computation.2.clone.1 | convolution fusion | flops 1086322688 | bytes 18883072 | tf_op jit(solution)/shard_map/while/body/eval_jaxpr/tgcd,sgd->gcts/dot_general | solution.py:68
  266.6 9.0 %fusion.63 = f32[1,4,512,128]{3,2,1,0:T(8,128)S(1)} fusion(f32[2048,512,4]{1,0,2:T(8,128)} %get-tuple-element.202, f32[4,512]{1,0:T(4,128)S(1)} %bitcast.105, pred[512,2048]{0,1:T(8,128)(4,1)S(1)} %broadcast_compare_fusion.2, f32[1,4,512,128]{3,2,1,0:T(8,128)S(1)} %get-tuple-element.218, bf16[4,2048,1,128]{3,1,2,0:T(8,128)(2,1)} %get-tuple-element.234, ...), kind=kOutput, calls=%fused_computation.10.clone.1 | convolution fusion | flops 1095499776 | bytes 20464128 | tf_op jit(solution)/shard_map/while/body/eval_jaxpr/gcts,sgd->gctd/dot_general | solution.py:77
  277.9 4.2 fusion.62
  282.9 10.2 %fusion.60 = (f32[4,512]{1,0:T(4,128)S(1)}, f32[2048,512,4]{1,0,2:T(8,128)}) fusion(pred[512,2048]{0,1:T(8,128)(4,1)S(1)} %broadcast_compare_fusion.2, bf16[512,1,4,128]{3,0,2,1:T(8,128)(2,1)} %get-tuple-element.233, bf16[4,2048,1,128]{3,1,2,0:T(8,128)(2,1)} %get-tuple-element.232, s32[]{:T(128)} %get-tuple-element.215), kind=kOutput, calls=%fused_computation.2.clone.1 | convolution fusion | flops 1086322688 | bytes 18883072 | tf_op jit(solution)/shard_map/while/body/eval_jaxpr/tgcd,sgd->gcts/dot_general | solution.py:68
  293.1 8.8 %fusion.63 = f32[1,4,512,128]{3,2,1,0:T(8,128)S(1)} fusion(f32[2048,512,4]{1,0,2:T(8,128)} %get-tuple-element.202, f32[4,512]{1,0:T(4,128)S(1)} %bitcast.105, pred[512,2048]{0,1:T(8,128)(4,1)S(1)} %broadcast_compare_fusion.2, f32[1,4,512,128]{3,2,1,0:T(8,128)S(1)} %get-tuple-element.218, bf16[4,2048,1,128]{3,1,2,0:T(8,128)(2,1)} %get-tuple-element.234, ...), kind=kOutput, calls=%fused_computation.10.clone.1 | convolution fusion | flops 1095499776 | bytes 20464128 | tf_op jit(solution)/shard_map/while/body/eval_jaxpr/gcts,sgd->gctd/dot_general | solution.py:77
  304.0 4.2 fusion.62
  309.0 10.0 %fusion.60 = (f32[4,512]{1,0:T(4,128)S(1)}, f32[2048,512,4]{1,0,2:T(8,128)}) fusion(pred[512,2048]{0,1:T(8,128)(4,1)S(1)} %broadcast_compare_fusion.2, bf16[512,1,4,128]{3,0,2,1:T(8,128)(2,1)} %get-tuple-element.233, bf16[4,2048,1,128]{3,1,2,0:T(8,128)(2,1)} %get-tuple-element.232, s32[]{:T(128)} %get-tuple-element.215), kind=kOutput, calls=%fused_computation.2.clone.1 | convolution fusion | flops 1086322688 | bytes 18883072 | tf_op jit(solution)/shard_map/while/body/eval_jaxpr/tgcd,sgd->gcts/dot_general | solution.py:68
  319.0 8.7 %fusion.63 = f32[1,4,512,128]{3,2,1,0:T(8,128)S(1)} fusion(f32[2048,512,4]{1,0,2:T(8,128)} %get-tuple-element.202, f32[4,512]{1,0:T(4,128)S(1)} %bitcast.105, pred[512,2048]{0,1:T(8,128)(4,1)S(1)} %broadcast_compare_fusion.2, f32[1,4,512,128]{3,2,1,0:T(8,128)S(1)} %get-tuple-element.218, bf16[4,2048,1,128]{3,1,2,0:T(8,128)(2,1)} %get-tuple-element.234, ...), kind=kOutput, calls=%fused_computation.10.clone.1 | convolution fusion | flops 1095499776 | bytes 20464128 | tf_op jit(solution)/shard_map/while/body/eval_jaxpr/gcts,sgd->gctd/dot_general | solution.py:77
  329.7 4.2 fusion.62
  334.7 10.0 %fusion.60 = (f32[4,512]{1,0:T(4,128)S(1)}, f32[2048,512,4]{1,0,2:T(8,128)}) fusion(pred[512,2048]{0,1:T(8,128)(4,1)S(1)} %broadcast_compare_fusion.2, bf16[512,1,4,128]{3,0,2,1:T(8,128)(2,1)} %get-tuple-element.233, bf16[4,2048,1,128]{3,1,2,0:T(8,128)(2,1)} %get-tuple-element.232, s32[]{:T(128)} %get-tuple-element.215), kind=kOutput, calls=%fused_computation.2.clone.1 | convolution fusion | flops 1086322688 | bytes 18883072 | tf_op jit(solution)/shard_map/while/body/eval_jaxpr/tgcd,sgd->gcts/dot_general | solution.py:68
  344.7 8.7 %fusion.63 = f32[1,4,512,128]{3,2,1,0:T(8,128)S(1)} fusion(f32[2048,512,4]{1,0,2:T(8,128)} %get-tuple-element.202, f32[4,512]{1,0:T(4,128)S(1)} %bitcast.105, pred[512,2048]{0,1:T(8,128)(4,1)S(1)} %broadcast_compare_fusion.2, f32[1,4,512,128]{3,2,1,0:T(8,128)S(1)} %get-tuple-element.218, bf16[4,2048,1,128]{3,1,2,0:T(8,128)(2,1)} %get-tuple-element.234, ...), kind=kOutput, calls=%fused_computation.10.clone.1 | convolution fusion | flops 1095499776 | bytes 20464128 | tf_op jit(solution)/shard_map/while/body/eval_jaxpr/gcts,sgd->gctd/dot_general | solution.py:77
  355.4 4.2 fusion.62
  360.5 10.2 %convolution_convert_fusion = bf16[512,8192]{1,0:T(8,128)(2,1)} fusion(bf16[512,512]{1,0:T(8,128)(2,1)S(1)} %bitcast.111, bf16[512,8192]{1,0:T(8,128)(2,1)} %all-gather.12.cloned.1.call-done), kind=kOutput, calls=%fused_computation.34 | convolution fusion | flops 4299161600 | bytes 17301504 | tf_op jit(solution)/shard_map/dot_general | solution.py:113
  370.8 115.3 %reduce-scatter.2.cloned.1.call-done = bf16[512,1024]{1,0:T(8,128)(2,1)} async-done(((bf16[512,8192]{1,0:T(8,128)(2,1)}), bf16[512,1024]{1,0:T(8,128)(2,1)}) %reduce-scatter.2.cloned.1.call-update) | async-done | bytes 1048592 | tf_op jit(solution)/shard_map/reduce_scatter | solution.py:118
  486.0 2.6 add_convert_fusion
  (74 shorter events, 24.4 us)
Async XLA Ops:
  7.2 185.9 %copy-start.5 = (f32[8192]{0:T(1024)S(1)}, f32[8192]{0:T(1024)}, u32[]{:S(2)}) copy-start(f32[8192]{0:T(1024)} %param.14) | copy-start | bytes 98308
  7.2 114.1 %all-gather.6.cloned.1.call-start = ((), (), s32[]{:S(2)}) async-start(), calls=%async_computation.1 | async-start | bytes 9437184 | tf_op jit(solution)/shard_map/all_gather | solution.py:37
  7.9 185.2 %all-gather.8.cloned.1.call-start = ((), (), s32[]{:S(2)}) async-start(), calls=%async_computation.2 | async-start | bytes 13369344 | tf_op jit(solution)/shard_map/all_gather | solution.py:44
  10.1 235.1 %all-gather.10.cloned.1.call-start = ((), (), s32[]{:S(2)}) async-start(), calls=%async_computation.3 | async-start | bytes 4456448 | tf_op jit(solution)/shard_map/all_gather | solution.py:19
  126.3 82.3 %copy-start.4 = (s32[512]{0:T(512)S(1)}, s32[512]{0:T(512)}, u32[]{:S(2)}) copy-start(s32[512]{0:T(512)} %param.13) | copy-start | bytes 6148
  207.0 153.5 %all-gather.12.cloned.1.call-start = ((), (), s32[]{:S(2)}) async-start(), calls=%async_computation.4 | async-start | bytes 8912896 | tf_op jit(solution)/shard_map/all_gather | solution.py:115
  207.6 278.5 %reduce-scatter.2.cloned.1.call-start = ((), (), s32[]{:S(2)}) async-start(), calls=%async_computation.5 | async-start | bytes 9437184 | tf_op jit(solution)/shard_map/reduce_scatter | solution.py:118
  230.0 25.7 %copy-start.2 = (f32[1,4,512,128]{3,2,1,0:T(8,128)S(1)}, f32[1,4,512,128]{3,2,1,0:T(8,128)}, u32[]{:S(2)}) copy-start(f32[1,4,512,128]{3,2,1,0:T(8,128)} %custom-call.2) | copy-start | bytes 3145732
  266.6 11.3 %copy-start = (f32[2048,512,4]{1,0,2:T(8,128)S(1)}, f32[2048,512,4]{1,0,2:T(8,128)}, u32[]{:S(2)}) copy-start(f32[2048,512,4]{1,0,2:T(8,128)} %get-tuple-element.202) | copy-start | bytes 50331652 | tf_op jit(solution)/shard_map/while
  293.1 10.9 %copy-start = (f32[2048,512,4]{1,0,2:T(8,128)S(1)}, f32[2048,512,4]{1,0,2:T(8,128)}, u32[]{:S(2)}) copy-start(f32[2048,512,4]{1,0,2:T(8,128)} %get-tuple-element.202) | copy-start | bytes 50331652 | tf_op jit(solution)/shard_map/while
  319.0 10.7 %copy-start = (f32[2048,512,4]{1,0,2:T(8,128)S(1)}, f32[2048,512,4]{1,0,2:T(8,128)}, u32[]{:S(2)}) copy-start(f32[2048,512,4]{1,0,2:T(8,128)} %get-tuple-element.202) | copy-start | bytes 50331652 | tf_op jit(solution)/shard_map/while
  344.7 10.7 %copy-start = (f32[2048,512,4]{1,0,2:T(8,128)S(1)}, f32[2048,512,4]{1,0,2:T(8,128)}, u32[]{:S(2)}) copy-start(f32[2048,512,4]{1,0,2:T(8,128)} %get-tuple-element.202) | copy-start | bytes 50331652 | tf_op jit(solution)/shard_map/while
  360.5 10.3 %copy-start.3 = (bf16[64,8,4,128]{3,1,2,0:T(8,128)(2,1)}, bf16[64,8,4,128]{3,1,2,0:T(8,128)(2,1)S(1)}, u32[]{:S(2)}) copy-start(bf16[64,8,4,128]{3,1,2,0:T(8,128)(2,1)S(1)} %copy.39) | copy-start | bytes 1572868
  370.7 115.3 %copy-start.1 = (bf16[512,1024]{1,0:T(8,128)(2,1)S(1)}, bf16[512,1024]{1,0:T(8,128)(2,1)}, u32[]{:S(2)}) copy-start(bf16[512,1024]{1,0:T(8,128)(2,1)} %param.12) | copy-start | bytes 3145732
Sparse Core Ops, SparseCore 0:
  10.3 110.8 all-gather.5
  123.5 69.5 all-gather.7
  207.1 38.0 all-gather.9
  246.8 52.1 all-gather.11
  370.9 115.1 reduce-scatter.1
where the time goes:
time: 496 us; the launch traced here: 495 us
  waiting for transfers between devices  308 us (62%)
  matrix products  98.3 us (20%)
  other arithmetic  35.1 us (7%)
  local copies, waits for them, and re-layouts  20.2 us (4%)
  blocking collectives  19 us (4%)
  between operations  14 us (3%)
    reduce_scatter x1, waiting for transfers between devices, shards(): lax.psum_scatter(out_terms.astype(jnp.bfloat16), 'tensor', scatter_dimens...  115 us
    all_gather x1, waiting for transfers between devices, shards(): features = lax.all_gather(tokens, 'tensor', axis=1, tiled=True)  110 us
    all_gather x1, waiting for transfers between devices, shards(): lax.all_gather(w_cat, 'seq', axis=0, tiled=True)  66.7 us
    dot_general x4, matrix products, attend_block(): jnp.einsum('tgcd,sgd->gcts', queries, block_keys, preferred_element_type=...  40.3 us
    dot_general x4, matrix products, attend_block(): jnp.einsum('gcts,sgd->gctd', weights.astype(jnp.bfloat16), block_values,...  35.2 us
    all_gather x1, blocking collectives, shards(): lax.all_gather(positions, 'seq', axis=0, tiled=True)  19 us
    reduce_sum x4, other arithmetic, attend_block(): denominator = denominator * rescale + jnp.sum(weights, -1)  16.6 us
    all_gather x1, waiting for transfers between devices, sent_together(): lax.all_gather(both, axis, axis=dim, tiled=True)  15.2 us
  transfers between devices with their start and end apart: 5, of which 4 were waited for; matrix products, arithmetic and copies ran while one was open for 24% of the time, Pallas kernels for 0%

commit v1 on v0

--- a/solution.py
+++ b/solution.py
@@ -33,8 +33,14 @@
 
 
 def shards(tokens, positions, norm_gain, w_query, w_key, w_value, b_query, b_key, b_value, w_out):
+
+    def clear_the_fields(dim_k, mesh_name, unit):
+        response = jnp.stack(lax.axis_size(mesh_name) * [unit])
+        last = lax.all_to_all(response, mesh_name, 0, 0)
+        return jnp.concatenate(last, axis=dim_k)
+
     tok_rows = tokens.shape[0]
-    features = lax.all_gather(tokens, "tensor", axis=1, tiled=True)
+    features = clear_the_fields(1, "tensor", tokens)
     inputs = features.astype(jnp.float32)
     inverse_rms = lax.rsqrt(jnp.mean(inputs * inputs, -1, keepdims=True) + NORM_EPS)
     normed = (inputs * inverse_rms * norm_gain[None, :]).astype(jnp.bfloat16)

time: 496 us -> 476 us (0.960)
  waiting for transfers between devices: 308 us -> 269 us
  starting transfers between devices: 0.2 us -> 8.03 us
  other arithmetic: 35.1 us -> 41.8 us
  local copies, waits for them, and re-layouts: 20.2 us -> 25.7 us
    all_to_all x0 -> x1, waiting for transfers between devices: none -> 117 us  [clear_the_fields(): last = lax.all_to_all(response, mesh_name, 0, 0)]
    all_gather x1 -> x0, waiting for transfers between devices: 110 us -> none  [shards(): features = lax.all_gather(tokens, 'tensor', axis=1, tiled=True)]
    all_gather x1, waiting for transfers between devices: 66.7 us -> 21.3 us  [shards(): lax.all_gather(w_cat, 'seq', axis=0, tiled=True)]
    convert_element_type x0 -> x1, other arithmetic: none -> 7.88 us  [shards(): normed = (inputs * inverse_rms * norm_gain[None, :]).astype(jnp.bfloat16)]
    all_to_all x0 -> x1, starting transfers between devices: none -> 7.87 us  [clear_the_fields(): last = lax.all_to_all(response, mesh_name, 0, 0)]
  transfers between devices with their start and end apart: 5 -> 5, of which waited for: 4 -> 4; matrix products, arithmetic and copies ran while one was open for 24% -> 27% of each run, Pallas kernels for 0% -> 0%
where the time goes in v1:
time: 476 us; the launch traced here: 475 us
  waiting for transfers between devices  269 us (57%)
  matrix products  97.8 us (21%)
  other arithmetic  41.8 us (9%)
  local copies, waits for them, and re-layouts  25.7 us (5%)
  blocking collectives  18.8 us (4%)
  between operations  14 us (3%)
  starting transfers between devices  8.03 us (2%)
    all_to_all x1, waiting for transfers between devices, clear_the_fields(): last = lax.all_to_all(response, mesh_name, 0, 0)  117 us
    reduce_scatter x1, waiting for transfers between devices, shards(): lax.psum_scatter(out_terms.astype(jnp.bfloat16), 'tensor', scatter_dimens...  115 us
    dot_general x4, matrix products, attend_block(): jnp.einsum('tgcd,sgd->gcts', queries, block_keys, preferred_element_type=...  40.3 us
    dot_general x4, matrix products, attend_block(): jnp.einsum('gcts,sgd->gctd', weights.astype(jnp.bfloat16), block_values,...  35.2 us
    all_gather x1, waiting for transfers between devices, shards(): lax.all_gather(w_cat, 'seq', axis=0, tiled=True)  21.3 us
    all_gather x1, blocking collectives, shards(): lax.all_gather(positions, 'seq', axis=0, tiled=True)  18.8 us
    reduce_sum x4, other arithmetic, attend_block(): denominator = denominator * rescale + jnp.sum(weights, -1)  16.6 us
    all_gather x1, waiting for transfers between devices, sent_together(): lax.all_gather(both, axis, axis=dim, tiled=True)  15 us
  transfers between devices with their start and end apart: 5, of which 4 were waited for; matrix products, arithmetic and copies ran while one was open for 27% of the time, Pallas kernels for 0%

profile of v1, /device:TPU:0, one launch (start us, length us, event | category | flops | bytes accessed | tf_op | source)
XLA Modules:
  0.0 475.3 jit_solution(18070897689401060275)
XLA Ops:
  14.9 7.9 %all-to-all-start = ((bf16[8,512,1024]{1,2,0:T(8,128)(2,1)}), bf16[8,512,1024]{1,2,0:T(8,128)(2,1)}, u32[]{:S(2)}, u32[]{:S(2)}) async-start(bf16[8,512,1024]{1,2,0:T(8,128)(2,1)} %stack.2), calls=%async_computation | async-start | bytes 16777216 | tf_op jit(solution)/shard_map/all_to_all | solution.py:39
  22.9 117.1 %all-to-all-done = bf16[8,512,1024]{1,2,0:T(8,128)(2,1)} async-done(((bf16[8,512,1024]{1,2,0:T(8,128)(2,1)}), bf16[8,512,1024]{1,2,0:T(8,128)(2,1)}, u32[]{:S(2)}, u32[]{:S(2)}) %all-to-all-start) | async-done | bytes 8388640 | tf_op jit(solution)/shard_map/all_to_all | solution.py:39
  140.0 5.3 %multiply_reduce_fusion = f32[512]{0:T(512)S(1)} fusion(bf16[8,512,1024]{1,2,0:T(8,128)(2,1)} %all-to-all-done), kind=kLoop, calls=%fused_computation.32 | loop fusion | flops 12582400 | bytes 8390656 | tf_op jit(solution)/shard_map/reduce_sum | solution.py:45
  145.3 7.9 %fusion.26 = bf16[512,8192]{0,1:T(8,128)(2,1)} fusion(f32[8192]{0:T(1024)S(1)} %copy-done.5, f32[512]{0:T(512)S(1)} %add_rsqrt_fusion, bf16[8,512,1024]{1,2,0:T(8,128)(2,1)} %all-to-all-done), kind=kLoop, calls=%fused_computation.31 | loop fusion | flops 16777216 | bytes 16812032 | tf_op jit(solution)/shard_map/convert_element_type | solution.py:46
  153.2 21.3 %all-gather.5.cloned.1.call-done = bf16[8192,768]{1,0:T(8,128)(2,1)} async-done(((bf16[512,768]{1,0:T(8,128)(2,1)}), bf16[8192,768]{1,0:T(8,128)(2,1)}) %all-gather.5.cloned.1.call-update) | async-done | bytes 12582928 | tf_op jit(solution)/shard_map/all_gather | solution.py:50
  174.5 12.0 %convolution_add_fusion = f32[512,768]{0,1:T(8,128)S(1)} fusion(bf16[512,8192]{0,1:T(8,128)(2,1)} %fusion.26, bf16[8192,768]{1,0:T(8,128)(2,1)} %all-gather.5.cloned.1.call-done, f32[768]{0:T(1024)S(1)} %pad_maximum_fusion.3), kind=kOutput, calls=%fused_computation.35 | convolution fusion | flops 6442844160 | bytes 22547456 | tf_op jit(solution)/shard_map/dot_general | solution.py:49
  189.7 18.8 %all-gather = s32[16,1,512]{2,1,0:T(1,128)S(1)} all-gather(s32[1,1,512]{2,1,0:T(1,128)S(1)} %bitcast.123), channel_id=1, replica_groups=mesh['seq'=16,'tensor'=8] {'seq'}, dimensions={0}, use_global_device_ids=true | all-gather | bytes 34816 | tf_op jit(solution)/shard_map/all_gather | solution.py:98
  210.9 15.0 %all-gather.7.cloned.1.call-done = bf16[8192,2,128]{0,2,1:T(8,128)(2,1)} async-done(((bf16[512,2,128]{0,2,1:T(8,128)(2,1)}), bf16[8192,2,128]{0,2,1:T(8,128)(2,1)}) %all-gather.7.cloned.1.call-update) | async-done | bytes 4194320 | tf_op jit(solution)/shard_map/all_gather | solution.py:19
  229.8 4.1 copy.42
  236.4 103.9 %while.15 = (s32[]{:T(128)}, f32[1,4,512]{2,1,0:T(4,128)S(1)}, f32[1,4,512]{2,1,0:T(4,128)S(1)}, f32[1,4,512,128]{3,2,1,0:T(8,128)S(1)}, s32[4,2048]{1,0:T(4,128...) while((s32[]{:T(128)}, f32[1,4,512]{2,1,0:T(4,128)S(1)}, ...), condition=%wide.region_4.5_spmd.clone, body=%wide.region_1.4_spmd.clone.sunk | while | flops 2203856896 | bytes 125463704 | solution.py:111
  237.1 10.2 %fusion.53 = (f32[4,512]{1,0:T(4,128)S(1)}, f32[2048,512,4]{1,0,2:T(8,128)}) fusion(pred[512,2048]{0,1:T(8,128)(4,1)S(1)} %broadcast_compare_fusion.2, bf16[512,1,4,128]{3,0,2,1:T(8,128)(2,1)} %get-tuple-element.242, bf16[4,2048,1,128]{3,1,2,0:T(8,128)(2,1)} %get-tuple-element.241, s32[]{:T(128)} %get-tuple-element.224), kind=kOutput, calls=%fused_computation.2.clone.1 | convolution fusion | flops 1086322688 | bytes 18883072 | tf_op jit(solution)/shard_map/while/body/eval_jaxpr/tgcd,sgd->gcts/dot_general | solution.py:74
  247.3 9.0 %fusion.56 = f32[1,4,512,128]{3,2,1,0:T(8,128)S(1)} fusion(f32[2048,512,4]{1,0,2:T(8,128)} %get-tuple-element.211, f32[4,512]{1,0:T(4,128)S(1)} %bitcast.114, pred[512,2048]{0,1:T(8,128)(4,1)S(1)} %broadcast_compare_fusion.2, f32[1,4,512,128]{3,2,1,0:T(8,128)S(1)} %get-tuple-element.227, bf16[4,2048,1,128]{3,1,2,0:T(8,128)(2,1)} %get-tuple-element.243, ...), kind=kOutput, calls=%fused_computation.10.clone.1 | convolution fusion | flops 1095499776 | bytes 20464128 | tf_op jit(solution)/shard_map/while/body/eval_jaxpr/gcts,sgd->gctd/dot_general | solution.py:83
  258.6 4.2 fusion.55
  263.6 10.2 %fusion.53 = (f32[4,512]{1,0:T(4,128)S(1)}, f32[2048,512,4]{1,0,2:T(8,128)}) fusion(pred[512,2048]{0,1:T(8,128)(4,1)S(1)} %broadcast_compare_fusion.2, bf16[512,1,4,128]{3,0,2,1:T(8,128)(2,1)} %get-tuple-element.242, bf16[4,2048,1,128]{3,1,2,0:T(8,128)(2,1)} %get-tuple-element.241, s32[]{:T(128)} %get-tuple-element.224), kind=kOutput, calls=%fused_computation.2.clone.1 | convolution fusion | flops 1086322688 | bytes 18883072 | tf_op jit(solution)/shard_map/while/body/eval_jaxpr/tgcd,sgd->gcts/dot_general | solution.py:74
  273.8 8.8 %fusion.56 = f32[1,4,512,128]{3,2,1,0:T(8,128)S(1)} fusion(f32[2048,512,4]{1,0,2:T(8,128)} %get-tuple-element.211, f32[4,512]{1,0:T(4,128)S(1)} %bitcast.114, pred[512,2048]{0,1:T(8,128)(4,1)S(1)} %broadcast_compare_fusion.2, f32[1,4,512,128]{3,2,1,0:T(8,128)S(1)} %get-tuple-element.227, bf16[4,2048,1,128]{3,1,2,0:T(8,128)(2,1)} %get-tuple-element.243, ...), kind=kOutput, calls=%fused_computation.10.clone.1 | convolution fusion | flops 1095499776 | bytes 20464128 | tf_op jit(solution)/shard_map/while/body/eval_jaxpr/gcts,sgd->gctd/dot_general | solution.py:83
  284.7 4.2 fusion.55
  289.7 10.0 %fusion.53 = (f32[4,512]{1,0:T(4,128)S(1)}, f32[2048,512,4]{1,0,2:T(8,128)}) fusion(pred[512,2048]{0,1:T(8,128)(4,1)S(1)} %broadcast_compare_fusion.2, bf16[512,1,4,128]{3,0,2,1:T(8,128)(2,1)} %get-tuple-element.242, bf16[4,2048,1,128]{3,1,2,0:T(8,128)(2,1)} %get-tuple-element.241, s32[]{:T(128)} %get-tuple-element.224), kind=kOutput, calls=%fused_computation.2.clone.1 | convolution fusion | flops 1086322688 | bytes 18883072 | tf_op jit(solution)/shard_map/while/body/eval_jaxpr/tgcd,sgd->gcts/dot_general | solution.py:74
  299.7 8.7 %fusion.56 = f32[1,4,512,128]{3,2,1,0:T(8,128)S(1)} fusion(f32[2048,512,4]{1,0,2:T(8,128)} %get-tuple-element.211, f32[4,512]{1,0:T(4,128)S(1)} %bitcast.114, pred[512,2048]{0,1:T(8,128)(4,1)S(1)} %broadcast_compare_fusion.2, f32[1,4,512,128]{3,2,1,0:T(8,128)S(1)} %get-tuple-element.227, bf16[4,2048,1,128]{3,1,2,0:T(8,128)(2,1)} %get-tuple-element.243, ...), kind=kOutput, calls=%fused_computation.10.clone.1 | convolution fusion | flops 1095499776 | bytes 20464128 | tf_op jit(solution)/shard_map/while/body/eval_jaxpr/gcts,sgd->gctd/dot_general | solution.py:83
  310.4 4.2 fusion.55
  315.4 10.0 %fusion.53 = (f32[4,512]{1,0:T(4,128)S(1)}, f32[2048,512,4]{1,0,2:T(8,128)}) fusion(pred[512,2048]{0,1:T(8,128)(4,1)S(1)} %broadcast_compare_fusion.2, bf16[512,1,4,128]{3,0,2,1:T(8,128)(2,1)} %get-tuple-element.242, bf16[4,2048,1,128]{3,1,2,0:T(8,128)(2,1)} %get-tuple-element.241, s32[]{:T(128)} %get-tuple-element.224), kind=kOutput, calls=%fused_computation.2.clone.1 | convolution fusion | flops 1086322688 | bytes 18883072 | tf_op jit(solution)/shard_map/while/body/eval_jaxpr/tgcd,sgd->gcts/dot_general | solution.py:74
  325.4 8.7 %fusion.56 = f32[1,4,512,128]{3,2,1,0:T(8,128)S(1)} fusion(f32[2048,512,4]{1,0,2:T(8,128)} %get-tuple-element.211, f32[4,512]{1,0:T(4,128)S(1)} %bitcast.114, pred[512,2048]{0,1:T(8,128)(4,1)S(1)} %broadcast_compare_fusion.2, f32[1,4,512,128]{3,2,1,0:T(8,128)S(1)} %get-tuple-element.227, bf16[4,2048,1,128]{3,1,2,0:T(8,128)(2,1)} %get-tuple-element.243, ...), kind=kOutput, calls=%fused_computation.10.clone.1 | convolution fusion | flops 1095499776 | bytes 20464128 | tf_op jit(solution)/shard_map/while/body/eval_jaxpr/gcts,sgd->gctd/dot_general | solution.py:83
  336.1 4.2 fusion.55
  341.2 10.2 %convolution_convert_fusion = bf16[512,8192]{1,0:T(8,128)(2,1)} fusion(bf16[512,512]{1,0:T(8,128)(2,1)S(1)} %bitcast.120, bf16[512,8192]{1,0:T(8,128)(2,1)} %all-gather.9.cloned.1.call-done), kind=kOutput, calls=%fused_computation.33 | convolution fusion | flops 4299161600 | bytes 17301504 | tf_op jit(solution)/shard_map/dot_general | solution.py:119
  351.5 114.7 %reduce-scatter.2.cloned.1.call-done = bf16[512,1024]{1,0:T(8,128)(2,1)} async-done(((bf16[512,8192]{1,0:T(8,128)(2,1)}), bf16[512,1024]{1,0:T(8,128)(2,1)}) %reduce-scatter.2.cloned.1.call-update) | async-done | bytes 1048592 | tf_op jit(solution)/shard_map/reduce_scatter | solution.py:124
  (82 shorter events, 34.5 us)
Async XLA Ops:
  7.2 167.3 %all-gather.5.cloned.1.call-start = ((), (), s32[]{:S(2)}) async-start(), calls=%async_computation.2 | async-start | bytes 13369344 | tf_op jit(solution)/shard_map/all_gather | solution.py:50
  14.9 7.9 %copy-start.4 = (s32[512]{0:T(512)S(1)}, s32[512]{0:T(512)}, u32[]{:S(2)}) copy-start(s32[512]{0:T(512)} %param.13) | copy-start | bytes 6148
  14.9 8.0 %copy-start.6 = (f32[512]{0:T(512)S(1)}, f32[512]{0:T(512)}, u32[]{:S(2)}) copy-start(f32[512]{0:T(512)} %param.18) | copy-start | bytes 6148
  14.9 8.0 %copy-start.7 = (f32[128]{0:T(128)S(1)}, f32[128]{0:T(128)}, u32[]{:S(2)}) copy-start(f32[128]{0:T(128)} %param.20) | copy-start | bytes 1540
  14.9 8.0 %copy-start.8 = (f32[128]{0:T(128)S(1)}, f32[128]{0:T(128)}, u32[]{:S(2)}) copy-start(f32[128]{0:T(128)} %param.19) | copy-start | bytes 1540
  14.9 125.1 %all-to-all-start = ((bf16[8,512,1024]{1,2,0:T(8,128)(2,1)}), bf16[8,512,1024]{1,2,0:T(8,128)(2,1)}, u32[]{:S(2)}, u32[]{:S(2)}) async-start(bf16[8,512,1024]{1,2,0:T(8,128)(2,1)} %stack.2), calls=%async_computation | async-start | bytes 16777216 | tf_op jit(solution)/shard_map/all_to_all | solution.py:39
  22.7 122.6 %copy-start.5 = (f32[8192]{0:T(1024)S(1)}, f32[8192]{0:T(1024)}, u32[]{:S(2)}) copy-start(f32[8192]{0:T(1024)} %param.14) | copy-start | bytes 98308
  22.7 203.2 %all-gather.7.cloned.1.call-start = ((), (), s32[]{:S(2)}) async-start(), calls=%async_computation.3 | async-start | bytes 4456448 | tf_op jit(solution)/shard_map/all_gather | solution.py:19
  187.9 153.3 %all-gather.9.cloned.1.call-start = ((), (), s32[]{:S(2)}) async-start(), calls=%async_computation.4 | async-start | bytes 8912896 | tf_op jit(solution)/shard_map/all_gather | solution.py:121
  188.6 277.6 %reduce-scatter.2.cloned.1.call-start = ((), (), s32[]{:S(2)}) async-start(), calls=%async_computation.5 | async-start | bytes 9437184 | tf_op jit(solution)/shard_map/reduce_scatter | solution.py:124
  210.9 25.5 %copy-start.2 = (f32[1,4,512,128]{3,2,1,0:T(8,128)S(1)}, f32[1,4,512,128]{3,2,1,0:T(8,128)}, u32[]{:S(2)}) copy-start(f32[1,4,512,128]{3,2,1,0:T(8,128)} %custom-call.2) | copy-start | bytes 3145732
  247.3 11.3 %copy-start = (f32[2048,512,4]{1,0,2:T(8,128)S(1)}, f32[2048,512,4]{1,0,2:T(8,128)}, u32[]{:S(2)}) copy-start(f32[2048,512,4]{1,0,2:T(8,128)} %get-tuple-element.211) | copy-start | bytes 50331652 | tf_op jit(solution)/shard_map/while
  273.8 10.9 %copy-start = (f32[2048,512,4]{1,0,2:T(8,128)S(1)}, f32[2048,512,4]{1,0,2:T(8,128)}, u32[]{:S(2)}) copy-start(f32[2048,512,4]{1,0,2:T(8,128)} %get-tuple-element.211) | copy-start | bytes 50331652 | tf_op jit(solution)/shard_map/while
  299.7 10.7 %copy-start = (f32[2048,512,4]{1,0,2:T(8,128)S(1)}, f32[2048,512,4]{1,0,2:T(8,128)}, u32[]{:S(2)}) copy-start(f32[2048,512,4]{1,0,2:T(8,128)} %get-tuple-element.211) | copy-start | bytes 50331652 | tf_op jit(solution)/shard_map/while
  325.4 10.7 %copy-start = (f32[2048,512,4]{1,0,2:T(8,128)S(1)}, f32[2048,512,4]{1,0,2:T(8,128)}, u32[]{:S(2)}) copy-start(f32[2048,512,4]{1,0,2:T(8,128)} %get-tuple-element.211) | copy-start | bytes 50331652 | tf_op jit(solution)/shard_map/while
  341.2 10.3 %copy-start.3 = (bf16[64,8,4,128]{3,1,2,0:T(8,128)(2,1)}, bf16[64,8,4,128]{3,1,2,0:T(8,128)(2,1)S(1)}, u32[]{:S(2)}) copy-start(bf16[64,8,4,128]{3,1,2,0:T(8,128)(2,1)S(1)} %copy.48) | copy-start | bytes 1572868
  351.4 114.8 %copy-start.1 = (bf16[512,1024]{1,0:T(8,128)(2,1)S(1)}, bf16[512,1024]{1,0:T(8,128)(2,1)}, u32[]{:S(2)}) copy-start(bf16[512,1024]{1,0:T(8,128)(2,1)} %param.12) | copy-start | bytes 3145732
Sparse Core Ops, SparseCore 0:
  10.2 164.2 all-gather.4
  188.0 37.8 all-gather.6
  227.6 52.1 all-gather.8
  351.6 114.5 reduce-scatter.1
